TPU v7x, 32 devices: a whole 2x2x4 slice. The times are simulated.
32 devices in a mesh: prow: 8 (over z, x), pcol: 4 (over y, core).
Axes of the slice: x: 2, y: 2, z: 4, core: 2. Of those that a mesh axis runs over, the one named last changes fastest.
Arguments:
- matrix: float32 [16384, 16384], P('prow', 'pcol'), may hold values from -6 to 6
Outputs:
- reduced: float32 [16384, 16384], P('prow', 'pcol')
- householder_coefficients: float32 [2, 8], replicated
All inputs are finite; a program needn't handle non-finite values.
Results may differ from a plain program's by a relative error of at most 0.0003.
Values sent between devices are 32-bit elements; how exact they have to be, the bound alone decides.
No kernel may reach another device: no remote copies, remote signals or barrier semaphores. Data moves between devices by JAX's collectives and lax.ppermute only.
A program may use at most 128 MiB of HBM per device.

v0:
```python
import jax
import jax.numpy as jnp
from jax import lax
from jax.sharding import PartitionSpec as P

NB = 8
epsilon = 1e-06


def from_root(x, axis, root):
    mine = lax.axis_index(axis) == root
    return lax.psum(jnp.where(mine, x, jnp.zeros_like(x)), axis)


def precise_dot(left, right):
    return jnp.dot(left, right, precision=lax.Precision.HIGHEST)


def inner_rows(left, right):
    return lax.dot_general(left, right, (((1,), (1,)), ((), ())), precision=lax.Precision.HIGHEST)


def householder(alpha_value, sumsq):
    norm_value = jnp.sqrt(sumsq + epsilon)
    signum = jnp.where(alpha_value >= 0.0, 1.0, -1.0).astype(jnp.float32)
    beta_value = -signum * norm_value
    return (beta_value, (beta_value - alpha_value) / beta_value, alpha_value - beta_value)


def per_device(matrix):
    rows_dev, cols_dev = matrix.shape
    prow_id = lax.axis_index("prow")
    pcol_id = lax.axis_index("pcol")
    row_glob = prow_id * rows_dev + jnp.arange(rows_dev, dtype=jnp.int32)
    col_glob = pcol_id * cols_dev + jnp.arange(cols_dev, dtype=jnp.int32)
    panel_index = jnp.arange(NB, dtype=jnp.int32)
    wide_index = jnp.arange(NB + 1, dtype=jnp.int32)
    held_tile = matrix
    source_side_factor_list = []
    target_side_factor_list = []
    column_owner_rank = 0 // cols_dev
    column_local_index = 0 - column_owner_rank * cols_dev
    row_root = 0 // rows_dev
    row_local = 0 - row_root * rows_dev
    col_panel = from_root(
        held_tile[:, column_local_index : column_local_index + NB + 1].T, "pcol", column_owner_rank
    )
    row_panel = from_root(held_tile[row_local : row_local + NB, :], "prow", row_root)
    sel_rows = (row_glob[None, :] == 0 + panel_index[:, None]).astype(jnp.float32)
    sel_cols = (col_glob[None, :] == 0 + wide_index[:, None]).astype(jnp.float32)
    v_rows = jnp.zeros((NB, rows_dev), jnp.float32)
    x_rows = jnp.zeros((NB, rows_dev), jnp.float32)
    y_cols = jnp.zeros((NB, cols_dev), jnp.float32)
    u_cols = jnp.zeros((NB, cols_dev), jnp.float32)
    v_panel = jnp.zeros((NB, NB), jnp.float32)
    y_panel = jnp.zeros((NB, NB + 1), jnp.float32)
    u_panel = jnp.zeros((NB, NB + 1), jnp.float32)
    diagonal_entries = []
    super_list = []
    for i in range(NB):
        column = (
            col_panel[i] - precise_dot(y_panel[:, i], v_rows) - precise_dot(u_panel[:, i], x_rows)
        )
        masked = jnp.where(row_glob >= i, column, 0.0)
        trans_part, v_coef, x_coef, col_window, col_sumsq, x_panel = lax.psum(
            (
                precise_dot(masked, held_tile),
                precise_dot(v_rows, masked),
                precise_dot(x_rows, masked),
                precise_dot(sel_rows, masked),
                jnp.sum(masked * masked),
                inner_rows(x_rows, sel_rows),
            ),
            "prow",
        )
        row_raw = row_panel[i]
        beta_left, source_side_coefficient, denom_left = householder(col_window[i], col_sumsq)
        row_eff = row_raw - precise_dot(v_panel[:, i], y_cols) - precise_dot(x_panel[:, i], u_cols)
        transposed = (
            trans_part
            - precise_dot(v_coef, y_cols)
            - precise_dot(x_coef, u_cols)
            - beta_left * row_eff
        ) / denom_left
        y_new = jnp.where(col_glob > i, source_side_coefficient * transposed, 0.0)
        v_new = (masked - beta_left * (row_glob == i).astype(jnp.float32)) / denom_left
        v_panel = v_panel.at[i].set(
            (col_window - beta_left * (panel_index == i).astype(jnp.float32)) / denom_left
        )
        v_rows = v_rows.at[i].set(v_new)
        y_cols = y_cols.at[i].set(y_new)
        row_new = row_eff - y_new
        row_masked = jnp.where(col_glob >= i + 1, row_new, 0.0)
        prod_part, y_coef, u_coef, row_window, row_sumsq, y_panel = lax.psum(
            (
                precise_dot(held_tile, row_masked),
                precise_dot(y_cols, row_masked),
                precise_dot(u_cols, row_masked),
                precise_dot(sel_cols, row_masked),
                jnp.sum(row_masked * row_masked),
                inner_rows(y_cols, sel_cols),
            ),
            "pcol",
        )
        right_reflector_beta, target_side_coefficient, denom_right = householder(
            row_window[i + 1], row_sumsq
        )
        column_next = (
            col_panel[i + 1]
            - precise_dot(y_panel[:, i + 1], v_rows)
            - precise_dot(u_panel[:, i + 1], x_rows)
        )
        product = (
            prod_part
            - precise_dot(y_coef, v_rows)
            - precise_dot(u_coef, x_rows)
            - right_reflector_beta * column_next
        ) / denom_right
        x_new = jnp.where(row_glob > i, target_side_coefficient * product, 0.0)
        u_new = (
            row_masked - right_reflector_beta * (col_glob == i + 1).astype(jnp.float32)
        ) / denom_right
        u_panel = u_panel.at[i].set(
            (row_window - right_reflector_beta * (wide_index == i + 1).astype(jnp.float32))
            / denom_right
        )
        x_rows = x_rows.at[i].set(x_new)
        u_cols = u_cols.at[i].set(u_new)
        diagonal_entries.append(beta_left)
        super_list.append(right_reflector_beta)
        source_side_factor_list.append(source_side_coefficient)
        target_side_factor_list.append(target_side_coefficient)
    stack_left = jnp.concatenate([v_rows, x_rows], axis=0)
    stack_right = jnp.concatenate([y_cols, u_cols], axis=0)
    updated = held_tile - lax.dot_general(
        stack_left, stack_right, (((0,), (0,)), ((), ())), precision=lax.Precision.HIGHEST
    )
    col_slice = updated[:, column_local_index : column_local_index + NB]
    col_keep = jnp.logical_and(pcol_id == column_owner_rank, row_glob >= NB)[:, None]
    updated = updated.at[:, column_local_index : column_local_index + NB].set(
        jnp.where(col_keep, v_rows.T, col_slice)
    )
    row_slice = updated[row_local : row_local + NB, :]
    panel_rows_glob = (0 + panel_index)[:, None]
    col_g = col_glob[None, :]
    v_window = jnp.where(panel_index[None, :] < panel_index[:, None], v_panel.T, 0.0)
    v_part = precise_dot(v_window, sel_cols[:NB])
    diag_arr = jnp.stack(diagonal_entries)[:, None]
    super_arr = jnp.stack(super_list)[:, None]
    panel_values = jnp.where(
        col_g < 0,
        row_slice,
        jnp.where(
            col_g < panel_rows_glob,
            v_part,
            jnp.where(
                col_g == panel_rows_glob,
                diag_arr,
                jnp.where(col_g == panel_rows_glob + 1, super_arr, u_cols),
            ),
        ),
    )
    row_final = jnp.where(prow_id == row_root, panel_values, row_slice)
    held_tile = updated.at[row_local : row_local + NB, :].set(row_final)
    householder_coefficients = jnp.stack(
        [jnp.stack(source_side_factor_list), jnp.stack(target_side_factor_list)]
    )
    return (held_tile, householder_coefficients)


def solution(mesh):
    in_specs = (P("prow", "pcol"),)
    out_specs = (P("prow", "pcol"), P())
    return jax.shard_map(
        per_device, mesh=mesh, in_specs=in_specs, out_specs=out_specs, check_vma=False
    )
```

profile of v0, /device:TPU:0, one launch (start us, length us, event | category | flops | bytes accessed | tf_op | source)
XLA Modules:
  0.0 1049.0 jit_solution(7705097731152169826)
XLA Ops:
  14.8 35.1 %all-reduce.25.cloned.1.call-done = f32[9,2048]{0,1:T(8,128)} async-done(((f32[9,2048]{0,1:T(8,128)}), f32[9,2048]{0,1:T(8,128)}) %all-reduce.25.cloned.1.call-update) | async-done | bytes 73744 | tf_op jit(solution)/shard_map/psum | solution.py:12
  60.9 19.6 %fusion.321 = f32[1,4096]{1,0:T(1,128)S(1)} fusion(f32[2048,1]{0,1:T(1,128)S(1)} %bitcast.809, f32[2048,4096]{1,0:T(8,128)} %param.99), kind=kOutput, calls=%fused_computation.530 | convolution fusion | flops 100663296 | bytes 33579008 | tf_op jit(solution)/shard_map/dot_general | solution.py:16
  80.7 38.6 %all-reduce.13 = (f32[8]{0:T(128)S(1)}, f32[4096]{0:T(1024)S(1)}, f32[8]{0:T(128)S(1)}, f32[]{:T(128)}, f32[8,8]{1,0:T(8,128)S(1)}) all-reduce(f32[8]{0:T(128)S(1)} %convolution_bitcast_fusion.45, f32[4096]{0:T(1024)S(1)} %bitcast.818, f32[8]{0:T(128)S(1)} %convolution_bitcast_fusion.46, ...), channel_id=1, replica_groups=mesh['prow'=8,'pcol'=4] {'prow'}, use_global_device_ids=true, to_apply=%region_5.6 | all-reduce | flops 4177 | bytes 33416 | tf_op jit(solution)/shard_map/psum | solution.py:65
  127.5 30.7 %fusion.322 = f32[1,2048]{1,0:T(1,128)S(1)} fusion(f32[4096,1]{0,1:T(1,128)S(1)} %bitcast.802, f32[2048,4096]{1,0:T(8,128)} %param.99), kind=kOutput, calls=%fused_computation.531 | convolution fusion | flops 100663296 | bytes 33579008 | tf_op jit(solution)/shard_map/dot_general | solution.py:16
  158.6 11.4 %all-reduce.21 = (f32[9]{0:T(128)S(1)}, f32[]{:T(128)}, f32[8,9]{1,0:T(8,128)S(1)}, f32[8]{0:T(128)S(1)}, f32[2048]{0:T(1024)S(1)}, /*index=5*/f32[8]{0:T(128)S(1)}) all-reduce(f32[9]{0:T(128)S(1)} %convolution_bitcast_fusion.44, f32[]{:T(128)} %get-tuple-element.757, ...), channel_id=1, replica_groups=mesh['prow'=8,'pcol'=4] {'pcol'}, use_global_device_ids=true, to_apply=%region_9.10 | all-reduce | flops 2146 | bytes 17168 | tf_op jit(solution)/shard_map/psum | solution.py:94
  177.3 19.5 %fusion.323 = f32[1,4096]{1,0:T(1,128)S(1)} fusion(f32[2048,1]{0,1:T(1,128)S(1)} %bitcast.805, f32[2048,4096]{1,0:T(8,128)} %param.99), kind=kOutput, calls=%fused_computation.532 | convolution fusion | flops 100663296 | bytes 33579008 | tf_op jit(solution)/shard_map/dot_general | solution.py:16
  197.5 36.5 %all-reduce.12 = (f32[8]{0:T(128)S(1)}, f32[4096]{0:T(1024)S(1)}, f32[8]{0:T(128)S(1)}, f32[8]{0:T(128)S(1)}, f32[]{:T(128)}, /*index=5*/f32[8,8]{1,0:T(8,128)S(1)}) all-reduce(f32[8]{0:T(128)S(1)} %convolution_bitcast_fusion.40, f32[4096]{0:T(1024)S(1)} %bitcast.813, ...), channel_id=1, replica_groups=mesh['prow'=8,'pcol'=4] {'prow'}, use_global_device_ids=true, to_apply=%region_20.21 | all-reduce | flops 4185 | bytes 33480 | tf_op jit(solution)/shard_map/psum | solution.py:65
  240.9 30.7 %fusion.324 = f32[1,2048]{1,0:T(1,128)S(1)} fusion(f32[4096,1]{0,1:T(1,128)S(1)} %bitcast.774, f32[2048,4096]{1,0:T(8,128)} %param.99), kind=kOutput, calls=%fused_computation.533 | convolution fusion | flops 100663296 | bytes 33579008 | tf_op jit(solution)/shard_map/dot_general | solution.py:16
  272.0 11.2 %all-reduce.20 = (f32[9]{0:T(128)S(1)}, f32[]{:T(128)}, f32[8,9]{1,0:T(8,128)S(1)}, f32[8]{0:T(128)S(1)}, f32[2048]{0:T(1024)S(1)}, /*index=5*/f32[8]{0:T(128)S(1)}) all-reduce(f32[9]{0:T(128)S(1)} %convolution_bitcast_fusion.39, f32[]{:T(128)} %get-tuple-element.750, ...), channel_id=1, replica_groups=mesh['prow'=8,'pcol'=4] {'pcol'}, use_global_device_ids=true, to_apply=%region_23.24 | all-reduce | flops 2146 | bytes 17168 | tf_op jit(solution)/shard_map/psum | solution.py:94
  296.4 19.5 %fusion.325 = f32[1,4096]{1,0:T(1,128)S(1)} fusion(f32[2048,1]{0,1:T(1,128)S(1)} %bitcast.777, f32[2048,4096]{1,0:T(8,128)} %param.99), kind=kOutput, calls=%fused_computation.534 | convolution fusion | flops 100663296 | bytes 33579008 | tf_op jit(solution)/shard_map/dot_general | solution.py:16
  316.6 34.1 %all-reduce.11 = (f32[8]{0:T(128)S(1)}, f32[4096]{0:T(1024)S(1)}, f32[8]{0:T(128)S(1)}, f32[8]{0:T(128)S(1)}, f32[]{:T(128)}, /*index=5*/f32[8,8]{1,0:T(8,128)S(1)}) all-reduce(f32[8]{0:T(128)S(1)} %convolution_bitcast_fusion.35, f32[4096]{0:T(1024)S(1)} %bitcast.811, ...), channel_id=1, replica_groups=mesh['prow'=8,'pcol'=4] {'prow'}, use_global_device_ids=true, to_apply=%region_34.35 | all-reduce | flops 4185 | bytes 33480 | tf_op jit(solution)/shard_map/psum | solution.py:65
  358.3 30.7 %fusion.326 = f32[1,2048]{1,0:T(1,128)S(1)} fusion(f32[4096,1]{0,1:T(1,128)S(1)} %bitcast.754, f32[2048,4096]{1,0:T(8,128)} %param.99), kind=kOutput, calls=%fused_computation.535 | convolution fusion | flops 100663296 | bytes 33579008 | tf_op jit(solution)/shard_map/dot_general | solution.py:16
  413.6 19.5 %fusion.327 = f32[1,4096]{1,0:T(1,128)S(1)} fusion(f32[2048,1]{0,1:T(1,128)S(1)} %bitcast.785, f32[2048,4096]{1,0:T(8,128)} %param.99), kind=kOutput, calls=%fused_computation.536 | convolution fusion | flops 100663296 | bytes 33579008 | tf_op jit(solution)/shard_map/dot_general | solution.py:16
  433.8 34.1 %all-reduce.10 = (f32[8]{0:T(128)S(1)}, f32[4096]{0:T(1024)S(1)}, f32[8]{0:T(128)S(1)}, f32[8]{0:T(128)S(1)}, f32[]{:T(128)}, /*index=5*/f32[8,8]{1,0:T(8,128)S(1)}) all-reduce(f32[8]{0:T(128)S(1)} %convolution_bitcast_fusion.30, f32[4096]{0:T(1024)S(1)} %bitcast.814, ...), channel_id=1, replica_groups=mesh['prow'=8,'pcol'=4] {'prow'}, use_global_device_ids=true, to_apply=%region_48.49 | all-reduce | flops 4185 | bytes 33480 | tf_op jit(solution)/shard_map/psum | solution.py:65
  475.6 30.7 %fusion.328 = f32[1,2048]{1,0:T(1,128)S(1)} fusion(f32[4096,1]{0,1:T(1,128)S(1)} %bitcast.758, f32[2048,4096]{1,0:T(8,128)} %param.99), kind=kOutput, calls=%fused_computation.537 | convolution fusion | flops 100663296 | bytes 33579008 | tf_op jit(solution)/shard_map/dot_general | solution.py:16
  506.6 11.2 %all-reduce.18 = (f32[9]{0:T(128)S(1)}, f32[]{:T(128)}, f32[8,9]{1,0:T(8,128)S(1)}, f32[8]{0:T(128)S(1)}, f32[2048]{0:T(1024)S(1)}, /*index=5*/f32[8]{0:T(128)S(1)}) all-reduce(f32[9]{0:T(128)S(1)} %convolution_bitcast_fusion.29, f32[]{:T(128)} %get-tuple-element.736, ...), channel_id=1, replica_groups=mesh['prow'=8,'pcol'=4] {'pcol'}, use_global_device_ids=true, to_apply=%region_51.52 | all-reduce | flops 2146 | bytes 17168 | tf_op jit(solution)/shard_map/psum | solution.py:94
  530.8 19.5 %fusion.329 = f32[1,4096]{1,0:T(1,128)S(1)} fusion(f32[2048,1]{0,1:T(1,128)S(1)} %bitcast.789, f32[2048,4096]{1,0:T(8,128)} %param.99), kind=kOutput, calls=%fused_computation.538 | convolution fusion | flops 100663296 | bytes 33579008 | tf_op jit(solution)/shard_map/dot_general | solution.py:16
  550.9 34.1 %all-reduce.9 = (f32[8]{0:T(128)S(1)}, f32[4096]{0:T(1024)S(1)}, f32[8]{0:T(128)S(1)}, f32[8]{0:T(128)S(1)}, f32[]{:T(128)}, /*index=5*/f32[8,8]{1,0:T(8,128)S(1)}) all-reduce(f32[8]{0:T(128)S(1)} %convolution_bitcast_fusion.25, f32[4096]{0:T(1024)S(1)} %bitcast.815, ...), channel_id=1, replica_groups=mesh['prow'=8,'pcol'=4] {'prow'}, use_global_device_ids=true, to_apply=%region_62.63 | all-reduce | flops 4185 | bytes 33480 | tf_op jit(solution)/shard_map/psum | solution.py:65
  592.4 30.7 %fusion.330 = f32[1,2048]{1,0:T(1,128)S(1)} fusion(f32[4096,1]{0,1:T(1,128)S(1)} %bitcast.762, f32[2048,4096]{1,0:T(8,128)} %param.99), kind=kOutput, calls=%fused_computation.539 | convolution fusion | flops 100663296 | bytes 33579008 | tf_op jit(solution)/shard_map/dot_general | solution.py:16
  623.4 11.2 %all-reduce.17 = (f32[9]{0:T(128)S(1)}, f32[]{:T(128)}, f32[8,9]{1,0:T(8,128)S(1)}, f32[8]{0:T(128)S(1)}, f32[2048]{0:T(1024)S(1)}, /*index=5*/f32[8]{0:T(128)S(1)}) all-reduce(f32[9]{0:T(128)S(1)} %convolution_bitcast_fusion.24, f32[]{:T(128)} %get-tuple-element.729, ...), channel_id=1, replica_groups=mesh['prow'=8,'pcol'=4] {'pcol'}, use_global_device_ids=true, to_apply=%region_65.66 | all-reduce | flops 2146 | bytes 17168 | tf_op jit(solution)/shard_map/psum | solution.py:94
  647.9 19.5 %fusion.331 = f32[1,4096]{1,0:T(1,128)S(1)} fusion(f32[2048,1]{0,1:T(1,128)S(1)} %bitcast.793, f32[2048,4096]{1,0:T(8,128)} %param.99), kind=kOutput, calls=%fused_computation.540 | convolution fusion | flops 100663296 | bytes 33579008 | tf_op jit(solution)/shard_map/dot_general | solution.py:16
  668.1 34.1 %all-reduce.8 = (f32[8]{0:T(128)S(1)}, f32[4096]{0:T(1024)S(1)}, f32[8]{0:T(128)S(1)}, f32[8]{0:T(128)S(1)}, f32[]{:T(128)}, /*index=5*/f32[8,8]{1,0:T(8,128)S(1)}) all-reduce(f32[8]{0:T(128)S(1)} %convolution_bitcast_fusion.20, f32[4096]{0:T(1024)S(1)} %bitcast.816, ...), channel_id=1, replica_groups=mesh['prow'=8,'pcol'=4] {'prow'}, use_global_device_ids=true, to_apply=%region_76.77 | all-reduce | flops 4185 | bytes 33480 | tf_op jit(solution)/shard_map/psum | solution.py:65
  710.1 30.7 %fusion.332 = f32[1,2048]{1,0:T(1,128)S(1)} fusion(f32[4096,1]{0,1:T(1,128)S(1)} %bitcast.766, f32[2048,4096]{1,0:T(8,128)} %param.99), kind=kOutput, calls=%fused_computation.541 | convolution fusion | flops 100663296 | bytes 33579008 | tf_op jit(solution)/shard_map/dot_general | solution.py:16
  741.1 11.2 %all-reduce.16 = (f32[9]{0:T(128)S(1)}, f32[]{:T(128)}, f32[8,9]{1,0:T(8,128)S(1)}, f32[8]{0:T(128)S(1)}, f32[2048]{0:T(1024)S(1)}, /*index=5*/f32[8]{0:T(128)S(1)}) all-reduce(f32[9]{0:T(128)S(1)} %convolution_bitcast_fusion.19, f32[]{:T(128)} %get-tuple-element.722, ...), channel_id=1, replica_groups=mesh['prow'=8,'pcol'=4] {'pcol'}, use_global_device_ids=true, to_apply=%region_79.80 | all-reduce | flops 2146 | bytes 17168 | tf_op jit(solution)/shard_map/psum | solution.py:94
  765.4 19.5 %fusion.333 = f32[1,4096]{1,0:T(1,128)S(1)} fusion(f32[2048,1]{0,1:T(1,128)S(1)} %bitcast.797, f32[2048,4096]{1,0:T(8,128)} %param.99), kind=kOutput, calls=%fused_computation.542 | convolution fusion | flops 100663296 | bytes 33579008 | tf_op jit(solution)/shard_map/dot_general | solution.py:16
  785.5 34.1 %all-reduce.7 = (f32[8]{0:T(128)S(1)}, f32[4096]{0:T(1024)S(1)}, f32[8]{0:T(128)S(1)}, f32[8]{0:T(128)S(1)}, f32[]{:T(128)}, /*index=5*/f32[8,8]{1,0:T(8,128)S(1)}) all-reduce(f32[8]{0:T(128)S(1)} %convolution_bitcast_fusion.15, f32[4096]{0:T(1024)S(1)} %bitcast.817, ...), channel_id=1, replica_groups=mesh['prow'=8,'pcol'=4] {'prow'}, use_global_device_ids=true, to_apply=%region_90.91 | all-reduce | flops 4185 | bytes 33480 | tf_op jit(solution)/shard_map/psum | solution.py:65
  827.1 30.7 %fusion.334 = f32[1,2048]{1,0:T(1,128)S(1)} fusion(f32[4096,1]{0,1:T(1,128)S(1)} %bitcast.750, f32[2048,4096]{1,0:T(8,128)} %param.99), kind=kOutput, calls=%fused_computation.543 | convolution fusion | flops 100663296 | bytes 33579008 | tf_op jit(solution)/shard_map/dot_general | solution.py:16
  858.1 11.2 %all-reduce.15 = (f32[9]{0:T(128)S(1)}, f32[]{:T(128)}, f32[8,9]{1,0:T(8,128)S(1)}, f32[8]{0:T(128)S(1)}, f32[2048]{0:T(1024)S(1)}, /*index=5*/f32[8]{0:T(128)S(1)}) all-reduce(f32[9]{0:T(128)S(1)} %convolution_bitcast_fusion.14, f32[]{:T(128)} %get-tuple-element.715, ...), channel_id=1, replica_groups=mesh['prow'=8,'pcol'=4] {'pcol'}, use_global_device_ids=true, to_apply=%region_93.94 | all-reduce | flops 2146 | bytes 17168 | tf_op jit(solution)/shard_map/psum | solution.py:94
  882.1 19.5 %fusion.335 = f32[1,4096]{1,0:T(1,128)S(1)} fusion(f32[2048,1]{0,1:T(1,128)S(1)} %bitcast.781, f32[2048,4096]{1,0:T(8,128)} %param.99), kind=kOutput, calls=%fused_computation.544 | convolution fusion | flops 100663296 | bytes 33579008 | tf_op jit(solution)/shard_map/dot_general | solution.py:16
  902.3 34.0 %all-reduce.6 = (f32[8]{0:T(128)S(1)}, f32[4096]{0:T(1024)S(1)}, f32[8]{0:T(128)S(1)}, f32[8]{0:T(128)S(1)}, f32[]{:T(128)}, /*index=5*/f32[8,8]{1,0:T(8,128)S(1)}) all-reduce(f32[8]{0:T(128)S(1)} %convolution_bitcast_fusion.10, f32[4096]{0:T(1024)S(1)} %bitcast.812, ...), channel_id=1, replica_groups=mesh['prow'=8,'pcol'=4] {'prow'}, use_global_device_ids=true, to_apply=%region_105.106 | all-reduce | flops 4185 | bytes 33480 | tf_op jit(solution)/shard_map/psum | solution.py:65
  943.6 30.7 %fusion.336 = f32[1,2048]{1,0:T(1,128)S(1)} fusion(f32[4096,1]{0,1:T(1,128)S(1)} %bitcast.770, f32[2048,4096]{1,0:T(8,128)} %param.99), kind=kOutput, calls=%fused_computation.545 | convolution fusion | flops 100663296 | bytes 33579008 | tf_op jit(solution)/shard_map/dot_general | solution.py:16
  997.8 32.9 %convolution_subtract_fusion = f32[2048,4096]{1,0:T(8,128)} fusion(f32[2048,4096]{1,0:T(8,128)} %param.99, f32[8,4096]{1,0:T(8,128)S(1)} %scatter.239, f32[8,4096]{1,0:T(8,128)S(1)} %scatter.235, f32[8,2048]{1,0:T(8,128)S(1)} %scatter.236, f32[8,2048]{1,0:T(8,128)S(1)} %copy.27), kind=kOutput, calls=%fused_computation | convolution fusion | flops 1619099648 | bytes 67502080 | tf_op jit(solution)/shard_map/dot_general | solution.py:135
  (325 shorter events, 175.6 us)
Async XLA Ops:
  7.2 42.8 %all-reduce.25.cloned.1.call-start = ((), (), s32[]{:S(2)}) async-start(), calls=%async_computation | async-start | bytes 2097152 | tf_op jit(solution)/shard_map/psum | solution.py:12
  9.5 114.8 %all-reduce.27.cloned.1.call-start = ((), (), s32[]{:S(2)}) async-start(), calls=%async_computation.1 | async-start | bytes 262144 | tf_op jit(solution)/shard_map/psum | solution.py:12
  882.1 114.7 %copy-start.1 = (f32[2048]{0:T(1024)S(1)}, f32[2048]{0:T(1024)}, u32[]{:S(2)}) copy-start(f32[2048]{0:T(1024)} %get-tuple-element.590) | copy-start | bytes 24580
  997.7 32.9 %copy-start.2 = (pred[2048]{0:T(1024)(128)(4,1)S(1)}, pred[2048]{0:T(1024)(128)(4,1)}, u32[]{:S(2)}) copy-start(pred[2048]{0:T(1024)(128)(4,1)} %fusion.145) | copy-start | bytes 6148
  997.8 41.9 %copy-start = (pred[9,4096]{1,0:T(8,128)(4,1)S(1)}, pred[9,4096]{1,0:T(8,128)(4,1)}, u32[]{:S(2)}) copy-start(pred[9,4096]{1,0:T(8,128)(4,1)} %iota_compare_fusion) | copy-start | bytes 110596
  997.8 41.9 %copy-start.3 = (pred[4096]{0:T(1024)(128)(4,1)S(1)}, pred[4096]{0:T(1024)(128)(4,1)}, u32[]{:S(2)}) copy-start(pred[4096]{0:T(1024)(128)(4,1)} %fusion.94) | copy-start | bytes 12292
  997.8 41.9 %copy-start.4 = (s32[8]{0:T(128)S(1)}, s32[8]{0:T(128)}, u32[]{:S(2)}) copy-start(s32[8]{0:T(128)} %iota_add_fusion.2) | copy-start | bytes 100
Sparse Core Ops, SparseCore 0:
  10.9 38.9 all-reduce.24
  53.3 71.0 all-reduce.26
where the time goes:
time: 1060 us; the launch traced here: 1050 us
  matrix products  483 us (46%)
  blocking collectives  369 us (35%)
  local copies, waits for them, and re-layouts  80.7 us (8%)
  between operations  56.4 us (5%)
  waiting for transfers between devices  38 us (4%)
  other arithmetic  21.1 us (2%)
    dot_general x134, matrix products, precise_dot(): return jnp.dot(left, right, precision=lax.Precision.HIGHEST)  447 us
    psum x8, blocking collectives, per_device(): lax.psum((precise_dot(masked, held_tile), precise_dot(v_rows, masked), pr...  280 us
    psum x8, blocking collectives, per_device(): lax.psum((precise_dot(held_tile, row_masked), precise_dot(y_cols, row_mas...  89.6 us
    psum x2, waiting for transfers between devices, from_root(): return lax.psum(jnp.where(mine, x, jnp.zeros_like(x)), axis)  38 us
    scatter x9, local copies, waits for them, and re-layouts, per_device(): v_rows = v_rows.at[i].set(v_new)  33.3 us
    dot_general x1, matrix products, per_device(): lax.dot_general(stack_left, stack_right, (((0,), (0,)), ((), ())), precis...  32.9 us
  transfers between devices with their start and end apart: 2, of which 2 were waited for; matrix products, arithmetic and copies ran while one was open for 4% of the time, Pallas kernels for 0%

commit v1 on v0

--- a/solution.py
+++ b/solution.py
@@ -9,7 +9,7 @@
 
 def from_root(x, axis, root):
     mine = lax.axis_index(axis) == root
-    return lax.psum(jnp.where(mine, x, jnp.zeros_like(x)), axis)
+    return jnp.sum(lax.all_gather(jnp.where(mine, x, jnp.zeros_like(x)), axis), axis=0)
 
 
 def precise_dot(left, right):

time: 1060 us -> 1010 us (0.953)
  waiting for transfers between devices: 38 us -> 0.02 us
    psum x2 -> x0, waiting for transfers between devices: 38 us -> none  [from_root(): return lax.psum(jnp.where(mine, x, jnp.zeros_like(x)), axis)]
  transfers between devices with their start and end apart: 2 -> 1, of which waited for: 2 -> 0; matrix products, arithmetic and copies ran while one was open for 4% -> 3% of each run, Pallas kernels for 0% -> 0%
where the time goes in v1:
time: 1010 us; the launch traced here: 1000 us
  matrix products  484 us (48%)
  blocking collectives  376 us (37%)
  local copies, waits for them, and re-layouts  70.6 us (7%)
  between operations  54.2 us (5%)
  other arithmetic  19.4 us (2%)
    dot_general x134, matrix products, precise_dot(): return jnp.dot(left, right, precision=lax.Precision.HIGHEST)  447 us
    psum x8, blocking collectives, per_device(): lax.psum((precise_dot(masked, held_tile), precise_dot(v_rows, masked), pr...  277 us
    psum x8, blocking collectives, per_device(): lax.psum((precise_dot(held_tile, row_masked), precise_dot(y_cols, row_mas...  89.7 us
    scatter x9, local copies, waits for them, and re-layouts, per_device(): v_rows = v_rows.at[i].set(v_new)  33.3 us
    dot_general x1, matrix products, per_device(): lax.dot_general(stack_left, stack_right, (((0,), (0,)), ((), ())), precis...  32.8 us
  transfers between devices with their start and end apart: 1, of which 0 were waited for; matrix products, arithmetic and copies ran while one was open for 3% of the time, Pallas kernels for 0%

profile of v1, /device:TPU:0, one launch (start us, length us, event | category | flops | bytes accessed | tf_op | source)
XLA Modules:
  0.0 1003.3 jit_solution(11703961645701190652)
XLA Ops:
  20.6 19.6 %fusion.322 = f32[1,4096]{1,0:T(1,128)S(1)} fusion(f32[2048,1]{0,1:T(1,128)S(1)} %bitcast.821, f32[2048,4096]{1,0:T(8,128)} %param.99), kind=kOutput, calls=%fused_computation.523 | convolution fusion | flops 100663296 | bytes 33579008 | tf_op jit(solution)/shard_map/dot_general | solution.py:16
  40.8 38.8 %all-reduce.13 = (f32[8]{0:T(128)S(1)}, f32[4096]{0:T(1024)S(1)}, f32[8]{0:T(128)S(1)}, f32[]{:T(128)}, f32[8,8]{1,0:T(8,128)S(1)}) all-reduce(f32[8]{0:T(128)S(1)} %convolution_bitcast_fusion.45, f32[4096]{0:T(1024)S(1)} %bitcast.831, f32[8]{0:T(128)S(1)} %convolution_bitcast_fusion.46, ...), channel_id=1, replica_groups=mesh['prow'=8,'pcol'=4] {'prow'}, use_global_device_ids=true, to_apply=%region_5.6 | all-reduce | flops 4177 | bytes 33416 | tf_op jit(solution)/shard_map/psum | solution.py:65
  88.0 30.7 %fusion.323 = f32[1,2048]{1,0:T(1,128)S(1)} fusion(f32[4096,1]{0,1:T(1,128)S(1)} %bitcast.815, f32[2048,4096]{1,0:T(8,128)} %param.99), kind=kOutput, calls=%fused_computation.524 | convolution fusion | flops 100663296 | bytes 33579008 | tf_op jit(solution)/shard_map/dot_general | solution.py:16
  119.1 11.7 %all-reduce.21 = (f32[9]{0:T(128)S(1)}, f32[]{:T(128)}, f32[8,9]{1,0:T(8,128)S(1)}, f32[8]{0:T(128)S(1)}, f32[2048]{0:T(1024)S(1)}, /*index=5*/f32[8]{0:T(128)S(1)}) all-reduce(f32[9]{0:T(128)S(1)} %convolution_bitcast_fusion.44, f32[]{:T(128)} %get-tuple-element.748, ...), channel_id=1, replica_groups=mesh['prow'=8,'pcol'=4] {'pcol'}, use_global_device_ids=true, to_apply=%region_9.10 | all-reduce | flops 2146 | bytes 17168 | tf_op jit(solution)/shard_map/psum | solution.py:94
  137.8 19.5 %fusion.324 = f32[1,4096]{1,0:T(1,128)S(1)} fusion(f32[2048,1]{0,1:T(1,128)S(1)} %bitcast.818, f32[2048,4096]{1,0:T(8,128)} %param.99), kind=kOutput, calls=%fused_computation.525 | convolution fusion | flops 100663296 | bytes 33579008 | tf_op jit(solution)/shard_map/dot_general | solution.py:16
  157.9 34.0 %all-reduce.12 = (f32[8]{0:T(128)S(1)}, f32[4096]{0:T(1024)S(1)}, f32[8]{0:T(128)S(1)}, f32[8]{0:T(128)S(1)}, f32[]{:T(128)}, /*index=5*/f32[8,8]{1,0:T(8,128)S(1)}) all-reduce(f32[8]{0:T(128)S(1)} %convolution_bitcast_fusion.40, f32[4096]{0:T(1024)S(1)} %bitcast.826, ...), channel_id=1, replica_groups=mesh['prow'=8,'pcol'=4] {'prow'}, use_global_device_ids=true, to_apply=%region_20.21 | all-reduce | flops 4185 | bytes 33480 | tf_op jit(solution)/shard_map/psum | solution.py:65
  198.5 30.7 %fusion.325 = f32[1,2048]{1,0:T(1,128)S(1)} fusion(f32[4096,1]{0,1:T(1,128)S(1)} %bitcast.787, f32[2048,4096]{1,0:T(8,128)} %param.99), kind=kOutput, calls=%fused_computation.526 | convolution fusion | flops 100663296 | bytes 33579008 | tf_op jit(solution)/shard_map/dot_general | solution.py:16
  229.6 11.1 %all-reduce.20 = (f32[9]{0:T(128)S(1)}, f32[]{:T(128)}, f32[8,9]{1,0:T(8,128)S(1)}, f32[8]{0:T(128)S(1)}, f32[2048]{0:T(1024)S(1)}, /*index=5*/f32[8]{0:T(128)S(1)}) all-reduce(f32[9]{0:T(128)S(1)} %convolution_bitcast_fusion.39, f32[]{:T(128)} %get-tuple-element.741, ...), channel_id=1, replica_groups=mesh['prow'=8,'pcol'=4] {'pcol'}, use_global_device_ids=true, to_apply=%region_23.24 | all-reduce | flops 2146 | bytes 17168 | tf_op jit(solution)/shard_map/psum | solution.py:94
  253.7 19.5 %fusion.326 = f32[1,4096]{1,0:T(1,128)S(1)} fusion(f32[2048,1]{0,1:T(1,128)S(1)} %bitcast.790, f32[2048,4096]{1,0:T(8,128)} %param.99), kind=kOutput, calls=%fused_computation.527 | convolution fusion | flops 100663296 | bytes 33579008 | tf_op jit(solution)/shard_map/dot_general | solution.py:16
  273.9 34.0 %all-reduce.11 = (f32[8]{0:T(128)S(1)}, f32[4096]{0:T(1024)S(1)}, f32[8]{0:T(128)S(1)}, f32[8]{0:T(128)S(1)}, f32[]{:T(128)}, /*index=5*/f32[8,8]{1,0:T(8,128)S(1)}) all-reduce(f32[8]{0:T(128)S(1)} %convolution_bitcast_fusion.35, f32[4096]{0:T(1024)S(1)} %bitcast.824, ...), channel_id=1, replica_groups=mesh['prow'=8,'pcol'=4] {'prow'}, use_global_device_ids=true, to_apply=%region_34.35 | all-reduce | flops 4185 | bytes 33480 | tf_op jit(solution)/shard_map/psum | solution.py:65
  315.3 30.7 %fusion.327 = f32[1,2048]{1,0:T(1,128)S(1)} fusion(f32[4096,1]{0,1:T(1,128)S(1)} %bitcast.767, f32[2048,4096]{1,0:T(8,128)} %param.99), kind=kOutput, calls=%fused_computation.528 | convolution fusion | flops 100663296 | bytes 33579008 | tf_op jit(solution)/shard_map/dot_general | solution.py:16
  346.3 11.1 %all-reduce.19 = (f32[9]{0:T(128)S(1)}, f32[]{:T(128)}, f32[8,9]{1,0:T(8,128)S(1)}, f32[8]{0:T(128)S(1)}, f32[2048]{0:T(1024)S(1)}, /*index=5*/f32[8]{0:T(128)S(1)}) all-reduce(f32[9]{0:T(128)S(1)} %convolution_bitcast_fusion.34, f32[]{:T(128)} %get-tuple-element.734, ...), channel_id=1, replica_groups=mesh['prow'=8,'pcol'=4] {'pcol'}, use_global_device_ids=true, to_apply=%region_37.38 | all-reduce | flops 2146 | bytes 17168 | tf_op jit(solution)/shard_map/psum | solution.py:94
  370.2 19.5 %fusion.328 = f32[1,4096]{1,0:T(1,128)S(1)} fusion(f32[2048,1]{0,1:T(1,128)S(1)} %bitcast.798, f32[2048,4096]{1,0:T(8,128)} %param.99), kind=kOutput, calls=%fused_computation.529 | convolution fusion | flops 100663296 | bytes 33579008 | tf_op jit(solution)/shard_map/dot_general | solution.py:16
  390.4 34.0 %all-reduce.10 = (f32[8]{0:T(128)S(1)}, f32[4096]{0:T(1024)S(1)}, f32[8]{0:T(128)S(1)}, f32[8]{0:T(128)S(1)}, f32[]{:T(128)}, /*index=5*/f32[8,8]{1,0:T(8,128)S(1)}) all-reduce(f32[8]{0:T(128)S(1)} %convolution_bitcast_fusion.30, f32[4096]{0:T(1024)S(1)} %bitcast.827, ...), channel_id=1, replica_groups=mesh['prow'=8,'pcol'=4] {'prow'}, use_global_device_ids=true, to_apply=%region_48.49 | all-reduce | flops 4185 | bytes 33480 | tf_op jit(solution)/shard_map/psum | solution.py:65
  431.6 30.7 %fusion.329 = f32[1,2048]{1,0:T(1,128)S(1)} fusion(f32[4096,1]{0,1:T(1,128)S(1)} %bitcast.771, f32[2048,4096]{1,0:T(8,128)} %param.99), kind=kOutput, calls=%fused_computation.530 | convolution fusion | flops 100663296 | bytes 33579008 | tf_op jit(solution)/shard_map/dot_general | solution.py:16
  462.6 11.1 %all-reduce.18 = (f32[9]{0:T(128)S(1)}, f32[]{:T(128)}, f32[8,9]{1,0:T(8,128)S(1)}, f32[8]{0:T(128)S(1)}, f32[2048]{0:T(1024)S(1)}, /*index=5*/f32[8]{0:T(128)S(1)}) all-reduce(f32[9]{0:T(128)S(1)} %convolution_bitcast_fusion.29, f32[]{:T(128)} %get-tuple-element.727, ...), channel_id=1, replica_groups=mesh['prow'=8,'pcol'=4] {'pcol'}, use_global_device_ids=true, to_apply=%region_51.52 | all-reduce | flops 2146 | bytes 17168 | tf_op jit(solution)/shard_map/psum | solution.py:94
  487.0 19.5 %fusion.330 = f32[1,4096]{1,0:T(1,128)S(1)} fusion(f32[2048,1]{0,1:T(1,128)S(1)} %bitcast.802, f32[2048,4096]{1,0:T(8,128)} %param.99), kind=kOutput, calls=%fused_computation.531 | convolution fusion | flops 100663296 | bytes 33579008 | tf_op jit(solution)/shard_map/dot_general | solution.py:16
  507.2 34.0 %all-reduce.9 = (f32[8]{0:T(128)S(1)}, f32[4096]{0:T(1024)S(1)}, f32[8]{0:T(128)S(1)}, f32[8]{0:T(128)S(1)}, f32[]{:T(128)}, /*index=5*/f32[8,8]{1,0:T(8,128)S(1)}) all-reduce(f32[8]{0:T(128)S(1)} %convolution_bitcast_fusion.25, f32[4096]{0:T(1024)S(1)} %bitcast.828, ...), channel_id=1, replica_groups=mesh['prow'=8,'pcol'=4] {'prow'}, use_global_device_ids=true, to_apply=%region_62.63 | all-reduce | flops 4185 | bytes 33480 | tf_op jit(solution)/shard_map/psum | solution.py:65
  548.6 30.7 %fusion.331 = f32[1,2048]{1,0:T(1,128)S(1)} fusion(f32[4096,1]{0,1:T(1,128)S(1)} %bitcast.775, f32[2048,4096]{1,0:T(8,128)} %param.99), kind=kOutput, calls=%fused_computation.532 | convolution fusion | flops 100663296 | bytes 33579008 | tf_op jit(solution)/shard_map/dot_general | solution.py:16
  579.6 11.1 %all-reduce.17 = (f32[9]{0:T(128)S(1)}, f32[]{:T(128)}, f32[8,9]{1,0:T(8,128)S(1)}, f32[8]{0:T(128)S(1)}, f32[2048]{0:T(1024)S(1)}, /*index=5*/f32[8]{0:T(128)S(1)}) all-reduce(f32[9]{0:T(128)S(1)} %convolution_bitcast_fusion.24, f32[]{:T(128)} %get-tuple-element.720, ...), channel_id=1, replica_groups=mesh['prow'=8,'pcol'=4] {'pcol'}, use_global_device_ids=true, to_apply=%region_65.66 | all-reduce | flops 2146 | bytes 17168 | tf_op jit(solution)/shard_map/psum | solution.py:94
  603.5 19.5 %fusion.332 = f32[1,4096]{1,0:T(1,128)S(1)} fusion(f32[2048,1]{0,1:T(1,128)S(1)} %bitcast.806, f32[2048,4096]{1,0:T(8,128)} %param.99), kind=kOutput, calls=%fused_computation.533 | convolution fusion | flops 100663296 | bytes 33579008 | tf_op jit(solution)/shard_map/dot_general | solution.py:16
  623.7 34.0 %all-reduce.8 = (f32[8]{0:T(128)S(1)}, f32[4096]{0:T(1024)S(1)}, f32[8]{0:T(128)S(1)}, f32[8]{0:T(128)S(1)}, f32[]{:T(128)}, /*index=5*/f32[8,8]{1,0:T(8,128)S(1)}) all-reduce(f32[8]{0:T(128)S(1)} %convolution_bitcast_fusion.20, f32[4096]{0:T(1024)S(1)} %bitcast.829, ...), channel_id=1, replica_groups=mesh['prow'=8,'pcol'=4] {'prow'}, use_global_device_ids=true, to_apply=%region_76.77 | all-reduce | flops 4185 | bytes 33480 | tf_op jit(solution)/shard_map/psum | solution.py:65
  664.9 30.7 %fusion.333 = f32[1,2048]{1,0:T(1,128)S(1)} fusion(f32[4096,1]{0,1:T(1,128)S(1)} %bitcast.779, f32[2048,4096]{1,0:T(8,128)} %param.99), kind=kOutput, calls=%fused_computation.534 | convolution fusion | flops 100663296 | bytes 33579008 | tf_op jit(solution)/shard_map/dot_general | solution.py:16
  695.9 11.1 %all-reduce.16 = (f32[9]{0:T(128)S(1)}, f32[]{:T(128)}, f32[8,9]{1,0:T(8,128)S(1)}, f32[8]{0:T(128)S(1)}, f32[2048]{0:T(1024)S(1)}, /*index=5*/f32[8]{0:T(128)S(1)}) all-reduce(f32[9]{0:T(128)S(1)} %convolution_bitcast_fusion.19, f32[]{:T(128)} %get-tuple-element.713, ...), channel_id=1, replica_groups=mesh['prow'=8,'pcol'=4] {'pcol'}, use_global_device_ids=true, to_apply=%region_79.80 | all-reduce | flops 2146 | bytes 17168 | tf_op jit(solution)/shard_map/psum | solution.py:94
  720.0 19.5 %fusion.334 = f32[1,4096]{1,0:T(1,128)S(1)} fusion(f32[2048,1]{0,1:T(1,128)S(1)} %bitcast.810, f32[2048,4096]{1,0:T(8,128)} %param.99), kind=kOutput, calls=%fused_computation.535 | convolution fusion | flops 100663296 | bytes 33579008 | tf_op jit(solution)/shard_map/dot_general | solution.py:16
  740.1 34.0 %all-reduce.7 = (f32[8]{0:T(128)S(1)}, f32[4096]{0:T(1024)S(1)}, f32[8]{0:T(128)S(1)}, f32[8]{0:T(128)S(1)}, f32[]{:T(128)}, /*index=5*/f32[8,8]{1,0:T(8,128)S(1)}) all-reduce(f32[8]{0:T(128)S(1)} %convolution_bitcast_fusion.15, f32[4096]{0:T(1024)S(1)} %bitcast.830, ...), channel_id=1, replica_groups=mesh['prow'=8,'pcol'=4] {'prow'}, use_global_device_ids=true, to_apply=%region_90.91 | all-reduce | flops 4185 | bytes 33480 | tf_op jit(solution)/shard_map/psum | solution.py:65
  781.2 30.7 %fusion.335 = f32[1,2048]{1,0:T(1,128)S(1)} fusion(f32[4096,1]{0,1:T(1,128)S(1)} %bitcast.763, f32[2048,4096]{1,0:T(8,128)} %param.99), kind=kOutput, calls=%fused_computation.536 | convolution fusion | flops 100663296 | bytes 33579008 | tf_op jit(solution)/shard_map/dot_general | solution.py:16
  836.3 19.5 %fusion.336 = f32[1,4096]{1,0:T(1,128)S(1)} fusion(f32[2048,1]{0,1:T(1,128)S(1)} %bitcast.794, f32[2048,4096]{1,0:T(8,128)} %param.99), kind=kOutput, calls=%fused_computation.537 | convolution fusion | flops 100663296 | bytes 33579008 | tf_op jit(solution)/shard_map/dot_general | solution.py:16
  856.5 34.0 %all-reduce.6 = (f32[8]{0:T(128)S(1)}, f32[4096]{0:T(1024)S(1)}, f32[8]{0:T(128)S(1)}, f32[8]{0:T(128)S(1)}, f32[]{:T(128)}, /*index=5*/f32[8,8]{1,0:T(8,128)S(1)}) all-reduce(f32[8]{0:T(128)S(1)} %convolution_bitcast_fusion.10, f32[4096]{0:T(1024)S(1)} %bitcast.825, ...), channel_id=1, replica_groups=mesh['prow'=8,'pcol'=4] {'prow'}, use_global_device_ids=true, to_apply=%region_105.106 | all-reduce | flops 4185 | bytes 33480 | tf_op jit(solution)/shard_map/psum | solution.py:65
  897.9 30.7 %fusion.337 = f32[1,2048]{1,0:T(1,128)S(1)} fusion(f32[4096,1]{0,1:T(1,128)S(1)} %bitcast.783, f32[2048,4096]{1,0:T(8,128)} %param.99), kind=kOutput, calls=%fused_computation.538 | convolution fusion | flops 100663296 | bytes 33579008 | tf_op jit(solution)/shard_map/dot_general | solution.py:16
  929.0 11.1 %all-reduce.14 = (f32[9]{0:T(128)S(1)}, f32[]{:T(128)}, f32[8,9]{1,0:T(8,128)S(1)}, f32[8]{0:T(128)S(1)}, f32[2048]{0:T(1024)S(1)}, /*index=5*/f32[8]{0:T(128)S(1)}) all-reduce(f32[9]{0:T(128)S(1)} %convolution_bitcast_fusion.9, f32[]{:T(128)} %get-tuple-element.699, ...), channel_id=1, replica_groups=mesh['prow'=8,'pcol'=4] {'pcol'}, use_global_device_ids=true, to_apply=%region_106.107 | all-reduce | flops 2146 | bytes 17168 | tf_op jit(solution)/shard_map/psum | solution.py:94
  952.4 32.8 %convolution_subtract_fusion = f32[2048,4096]{1,0:T(8,128)} fusion(f32[2048,4096]{1,0:T(8,128)} %param.99, f32[8,4096]{1,0:T(8,128)S(1)} %scatter.239, f32[8,4096]{1,0:T(8,128)S(1)} %scatter.235, f32[8,2048]{1,0:T(8,128)S(1)} %scatter.236, f32[8,2048]{1,0:T(8,128)S(1)} %copy.40), kind=kOutput, calls=%fused_computation | convolution fusion | flops 1619099648 | bytes 67502080 | tf_op jit(solution)/shard_map/dot_general | solution.py:135
  (327 shorter events, 158.5 us)
Async XLA Ops:
  7.2 77.9 %all-gather.5.cloned.1.call-start = ((), (), s32[]{:S(2)}) async-start(), calls=%async_computation | async-start | bytes 1179648 | tf_op jit(solution)/shard_map/all_gather | solution.py:12
  836.3 115.2 %copy-start.1 = (f32[1,2048]{1,0:T(1,128)S(1)}, f32[1,2048]{1,0:T(1,128)}, u32[]{:S(2)}) copy-start(f32[1,2048]{1,0:T(1,128)} %get-tuple-element.753) | copy-start | bytes 24580
  952.4 32.9 %copy-start.2 = (pred[2048]{0:T(1024)(128)(4,1)S(1)}, pred[2048]{0:T(1024)(128)(4,1)}, u32[]{:S(2)}) copy-start(pred[2048]{0:T(1024)(128)(4,1)} %fusion.145) | copy-start | bytes 6148
  952.4 41.8 %copy-start = (pred[9,4096]{1,0:T(8,128)(4,1)S(1)}, pred[9,4096]{1,0:T(8,128)(4,1)}, u32[]{:S(2)}) copy-start(pred[9,4096]{1,0:T(8,128)(4,1)} %iota_compare_fusion) | copy-start | bytes 110596
  952.4 41.8 %copy-start.3 = (pred[4096]{0:T(1024)(128)(4,1)S(1)}, pred[4096]{0:T(1024)(128)(4,1)}, u32[]{:S(2)}) copy-start(pred[4096]{0:T(1024)(128)(4,1)} %fusion.94) | copy-start | bytes 12292
  952.4 41.8 %copy-start.4 = (s32[8]{0:T(128)S(1)}, s32[8]{0:T(128)}, u32[]{:S(2)}) copy-start(s32[8]{0:T(128)} %iota_add_fusion.2) | copy-start | bytes 100
Sparse Core Ops, SparseCore 0:
  10.7 43.0 all-gather.4
